TPU v7x, 256 devices: a whole 4x4x8 slice. The times are simulated.
256 devices in a mesh: row: 16 (over y, z_hi), col: 16 (over x, z_lo, core).
Axes of the slice: x: 4, y: 4, z: 8 (z_hi: 4, z_lo: 2; z = z_hi * 2 + z_lo), core: 2. Of those that a mesh axis runs over, the one named last changes fastest.
Arguments:
- left_act: bfloat16 [1536, 128], P(('row', 'col')), may hold values from -540 to 540
- right_act: bfloat16 [1536, 128], P(('row', 'col')), may hold values from -6 to 6
- norm_gain: float32 [128], replicated, may hold values from 0.25 to 1.75
- norm_bias: float32 [128], replicated, may hold values from -3 to 3
- w_in: bfloat16 [128, 512], replicated, may hold values from -0.5 to 0.5
- b_in: float32 [512], replicated, may hold values from -3 to 3
- w_out: bfloat16 [512, 128], replicated, may hold values from -0.25 to 0.25
- w_bins: bfloat16 [128, 64], replicated, may hold values from -0.5 to 0.5
- labels: int32 [1536, 1536], P('row', 'col'), may hold values from 0 to 63, as said below
Outputs:
- grad_left: float32 [1536, 128], P(('row', 'col'))
- grad_right: float32 [1536, 128], P('col')
- grad_w_in: float32 [128, 512], replicated
- grad_w_out: float32 [512, 128], replicated
- grad_w_bins: float32 [128, 64], replicated
Inputs may be any that keep to these rules, and one draw needn't show every extreme that they name: labels is symmetric: labels[i, j] equals labels[j, i].
All inputs are finite; a program needn't handle non-finite values.
Results may differ from a plain program's by a relative error of at most 0.00039.
Values may be sent and summed in bfloat16 or wider, within the bound.
No kernel may reach another device: no remote copies, remote signals or barrier semaphores. Data moves between devices by JAX's collectives and lax.ppermute only.
A program may use at most 64 MiB of HBM per device.

v0:
```python
import jax
import jax.numpy as jnp
from jax import lax
from jax.sharding import PartitionSpec as P


def from_everyone(value, axis):
    count = lax.axis_size(axis)
    return lax.all_to_all(
        jnp.broadcast_to(value[None], (count, *value.shape)), axis, 0, 0, tiled=True
    )


def laid_out(pieces, dim):
    shape = list(pieces.shape[1:])
    shape[dim] *= pieces.shape[0]
    return jnp.moveaxis(pieces, 0, dim).reshape(shape)


def gather_directly(value, axis, dim):
    pieces = from_everyone(value, axis)
    return laid_out(pieces, dim)


def picked(value, axis, root):
    return lax.dynamic_index_in_dim(lax.all_gather(value, axis), root, 0, keepdims=False)


def over_copies(value, axis):
    return from_everyone(value, axis).sum(axis=0)


def inner(first, second):
    return lax.dot_general(
        first, second, (((0,), (0,)), ((), ())), preferred_element_type=jnp.float32
    )


def outer(first, second):
    return lax.dot_general(
        first, second, (((1,), (1,)), ((), ())), preferred_element_type=jnp.float32
    )


def transition(left_rows, right_cols, gain, bias, w_in, b_in, w_out):
    summed = (
        left_rows.astype(jnp.float32)[:, None, :] + right_cols.astype(jnp.float32)[None, :, :]
    ).reshape(-1, left_rows.shape[1])
    center = summed - jnp.mean(summed, axis=-1, keepdims=True)
    inv_scale = lax.rsqrt(jnp.mean(center * center, axis=-1, keepdims=True) + 1e-05)
    normal_form = center * inv_scale
    normed = (normal_form * gain + bias).astype(jnp.bfloat16)
    pre_act = jnp.dot(normed, w_in, preferred_element_type=jnp.float32) + b_in
    hidden = (pre_act * jax.nn.sigmoid(pre_act)).astype(jnp.bfloat16)
    updated = (summed + jnp.dot(hidden, w_out, preferred_element_type=jnp.float32)).astype(
        jnp.bfloat16
    )
    return (normal_form, inv_scale, normed, pre_act, hidden, updated)


def pair_backward(sym, bin_labels, parts, gain, w_in, w_out, w_bins):
    normal_form, inv_scale, normed, pre_act, hidden, updated = parts
    shifted = sym - jnp.max(sym, axis=-1, keepdims=True)
    expo = jnp.exp(shifted)
    probs = expo / jnp.sum(expo, axis=-1, keepdims=True)
    onehot = (bin_labels[..., None] == lax.iota(jnp.int32, sym.shape[-1])).astype(jnp.float32)
    logit_grad = (2.0 * (probs - onehot)).reshape(-1, sym.shape[-1]).astype(jnp.bfloat16)
    grad_bins = inner(updated, logit_grad)
    upd_grad = outer(logit_grad, w_bins)
    upd_half = upd_grad.astype(jnp.bfloat16)
    grad_out = inner(hidden, upd_half)
    hid_grad = outer(upd_half, w_out)
    sigma = jax.nn.sigmoid(pre_act)
    pre_grad = (hid_grad * sigma * (1.0 + pre_act * (1.0 - sigma))).astype(jnp.bfloat16)
    grad_in = inner(normed, pre_grad)
    norm_grad = outer(pre_grad, w_in) * gain
    pair_grad = (
        inv_scale
        * (
            norm_grad
            - jnp.mean(norm_grad, axis=-1, keepdims=True)
            - normal_form * jnp.mean(norm_grad * normal_form, axis=-1, keepdims=True)
        )
        + upd_grad
    )
    return (grad_in, grad_out, grad_bins, pair_grad)


def on_device(left_act, right_act, norm_gain, norm_bias, w_in, b_in, w_out, w_bins, labels):
    tile_rows, tile_cols = labels.shape
    width = left_act.shape[1]
    stacked = jnp.stack([left_act, right_act])
    row_block = gather_directly(stacked, "col", 1)
    fanout = lax.axis_size("row") // lax.axis_size("col")
    pieces = picked(row_block, "row", lax.axis_index("col") * fanout + 0)
    stride_rows = 8
    groups = tile_rows // stride_rows

    def advance(running, record):
        left_rows, right_rows, bin_labels = record
        own_parts = transition(left_rows, pieces[1], norm_gain, norm_bias, w_in, b_in, w_out)
        own_logits = jnp.dot(own_parts[5], w_bins, preferred_element_type=jnp.float32).reshape(
            stride_rows, tile_cols, -1
        )
        far_parts = transition(pieces[0], right_rows, norm_gain, norm_bias, w_in, b_in, w_out)
        far_logits = jnp.dot(far_parts[5], w_bins, preferred_element_type=jnp.float32).reshape(
            tile_cols, stride_rows, -1
        )
        sym = own_logits + jnp.transpose(far_logits, (1, 0, 2))
        grads = pair_backward(sym, bin_labels, own_parts, norm_gain, w_in, w_out, w_bins)
        pair_grad = grads[3].reshape(stride_rows, tile_cols, width)
        running = (
            running[0] + grads[0],
            running[1] + grads[1],
            running[2] + grads[2],
            running[3] + jnp.sum(pair_grad, axis=0),
        )
        return (running, jnp.sum(pair_grad, axis=1))

    start = (
        jnp.zeros((width, w_in.shape[1]), jnp.float32),
        jnp.zeros((w_in.shape[1], width), jnp.float32),
        jnp.zeros((width, w_bins.shape[1]), jnp.float32),
        jnp.zeros((tile_cols, width), jnp.float32),
    )
    records = (
        row_block[0].reshape(groups, stride_rows, width),
        row_block[1].reshape(groups, stride_rows, width),
        labels.reshape(groups, stride_rows, tile_cols),
    )
    running, left_terms = lax.scan(advance, start, records)
    grad_left = lax.psum_scatter(
        left_terms.reshape(tile_rows, width), "col", scatter_dimension=0, tiled=True
    )
    grad_right = over_copies(running[3], "row")
    grad_in, grad_out, grad_bins = lax.psum((running[0], running[1], running[2]), ("row", "col"))
    residues = tile_rows * lax.axis_size("row")
    return (grad_left, grad_right, grad_in / residues, grad_out / residues, grad_bins / residues)


def solution(mesh):
    placed = (
        P(("row", "col"), None),
        P(("row", "col"), None),
        P(),
        P(),
        P(),
        P(),
        P(),
        P(),
        P("row", "col"),
    )
    return jax.shard_map(
        on_device,
        mesh=mesh,
        in_specs=placed,
        out_specs=(P(("row", "col"), None), P("col", None), P(), P(), P()),
        check_vma=False,
    )
```

profile of v0, /device:TPU:2, one launch (start us, length us, event | category | flops | bytes accessed | tf_op | source)
XLA Modules:
  0.0 512.4 jit_solution(3659964022238284578)
XLA Ops:
  8.5 6.2 %all-to-all-start = ((bf16[16,2,6,128]{3,1,2,0:T(2,128)(2,1)}), bf16[16,2,6,128]{3,1,2,0:T(2,128)(2,1)S(1)}, u32[]{:S(2)}, u32[]{:S(2)}) async-start(bf16[16,2,6,128]{3,1,2,0:T(2,128)(2,1)} %broadcast_in_dim.22), calls=%async_computation | async-start | bytes 98304 | tf_op jit(solution)/shard_map/all_to_all | solution.py:9
  14.8 4.7 all-to-all-done
  19.8 52.6 %all_gather.3 = bf16[16,2,96,128]{3,2,1,0:T(8,128)(2,1)S(1)} all-gather(bf16[1,2,96,128]{3,2,1,0:T(8,128)(2,1)S(1)} %copy.34), channel_id=1, replica_groups=mesh['row'=16,'col'=16] {'row'}, dimensions={0}, use_global_device_ids=true | all-gather | bytes 835584 | tf_op jit(solution)/shard_map/all_gather | solution.py:26
  72.4 161.3 %while.19 = (s32[]{:T(128)}, f32[128,512]{1,0:T(8,128)S(1)}, f32[512,128]{1,0:T(8,128)S(1)}, f32[128,64]{0,1:T(8,128)S(1)}, f32[96,128]{1,0:T(8,128)S(1)}, /*ind...) while((s32[]{:T(128)}, f32[128,512]{1,0:T(8,128)S(1)}, ...), condition=%wide.region_11.12_spmd.clone, body=%wide.region_0.11_spmd.clone.sunk | while | flops 869032064 | bytes 20266860 | solution.py:131
  81.8 2.1 multiply_convert_fusion.6
  87.7 1.9 fusion.121
  95.2 2.1 multiply_convert_fusion.6
  108.6 2.1 multiply_convert_fusion.6
  114.5 1.9 fusion.121
  122.1 2.1 multiply_convert_fusion.6
  135.5 2.1 multiply_convert_fusion.6
  141.4 1.9 fusion.121
  149.0 2.1 multiply_convert_fusion.6
  162.4 2.1 multiply_convert_fusion.6
  168.3 1.9 fusion.121
  175.9 2.1 multiply_convert_fusion.6
  189.3 2.1 multiply_convert_fusion.6
  202.7 2.1 multiply_convert_fusion.6
  216.2 2.1 multiply_convert_fusion.6
  229.6 2.1 multiply_convert_fusion.6
  234.7 3.6 all-to-all-start.1
  239.7 55.0 %all-reduce = f32[96,128]{1,0:T(8,128)S(1)} all-reduce(f32[96,128]{1,0:T(8,128)S(1)} %bitcast.153), channel_id=2, replica_groups=mesh['row'=16,'col'=16] {'col'}, use_global_device_ids=true, to_apply=%region_12.13.clone | all-reduce | flops 12288 | bytes 98304
  295.3 79.4 %psum.23 = f32[128,64]{0,1:T(8,128)S(1)} all-reduce(f32[128,64]{0,1:T(8,128)S(1)} %get-tuple-element.95), channel_id=1, replica_groups=mesh['row'=16,'col'=16] {'row','col'}, use_global_device_ids=true, to_apply=%region_16.17 | all-reduce | flops 8192 | bytes 65536 | tf_op jit(solution)/shard_map/psum | solution.py:136
  375.3 126.2 %all-reduce.4.cloned.1.call-done = (f32[128,512]{1,0:T(8,128)}, f32[512,128]{1,0:T(8,128)}) async-done(((f32[128,512]{1,0:T(8,128)}, f32[512,128]{1,0:T(8,128)}), (f32[128,512]{1,0:T(8,128)}, f32[512,128]{1,0:T(8,128)})) %all-reduce.4.cloned.1.call-update) | async-done | bytes 524304 | tf_op jit(solution)/shard_map/psum | solution.py:136
  (613 shorter events, 133.8 us)
Async XLA Ops:
  8.5 10.9 %all-to-all-start = ((bf16[16,2,6,128]{3,1,2,0:T(2,128)(2,1)}), bf16[16,2,6,128]{3,1,2,0:T(2,128)(2,1)S(1)}, u32[]{:S(2)}, u32[]{:S(2)}) async-start(bf16[16,2,6,128]{3,1,2,0:T(2,128)(2,1)} %broadcast_in_dim.22), calls=%async_computation | async-start | bytes 98304 | tf_op jit(solution)/shard_map/all_to_all | solution.py:9
  74.2 2.7 copy-start.2
  87.6 2.7 copy-start.2
  87.6 2.7 copy-start.7
  101.1 2.7 copy-start.2
  114.5 2.7 copy-start.2
  114.5 2.7 copy-start.7
  128.0 2.7 copy-start.2
  141.4 2.7 copy-start.2
  141.4 2.7 copy-start.7
  154.9 2.7 copy-start.2
  168.3 2.7 copy-start.2
  168.3 2.7 copy-start.7
  181.7 2.7 copy-start.2
  195.2 2.7 copy-start.2
  195.2 2.7 copy-start.7
  208.6 2.7 copy-start.2
  222.1 2.7 copy-start.2
  222.1 2.7 copy-start.7
  233.7 6.0 %copy-start = (f32[512,128]{1,0:T(8,128)}, f32[512,128]{1,0:T(8,128)S(1)}, u32[]{:S(2)}) copy-start(f32[512,128]{1,0:T(8,128)S(1)} %get-tuple-element.94) | copy-start | bytes 786436
  233.7 6.0 %copy-start.1 = (f32[128,512]{1,0:T(8,128)}, f32[128,512]{1,0:T(8,128)S(1)}, u32[]{:S(2)}) copy-start(f32[128,512]{1,0:T(8,128)S(1)} %get-tuple-element.93) | copy-start | bytes 786436
  233.7 4.7 copy-start.8
  234.7 270.1 %all-to-all-start.1 = ((f32[16,96,128]{2,1,0:T(8,128)}), f32[16,96,128]{2,1,0:T(8,128)S(1)}, u32[]{:S(2)}, u32[]{:S(2)}) async-start(f32[16,96,128]{2,1,0:T(8,128)} %broadcast_in_dim.23), calls=%async_computation.1 | async-start | bytes 1572864 | tf_op jit(solution)/shard_map/all_to_all | solution.py:9
  238.4 263.2 %all-reduce.4.cloned.1.call-start = ((), (), s32[]{:S(2)}) async-start(), calls=%async_computation.2 | async-start | bytes 1048576 | tf_op jit(solution)/shard_map/psum | solution.py:136
  (54 other events, 118.5 us)
Sparse Core Ops, SparseCore 0:
  245.4 256.1 all-reduce.3
where the time goes:
time: 514 us; the launch traced here: 512 us
  blocking collectives  187 us (36%)
  waiting for transfers between devices  131 us (25%)
  matrix products  113 us (22%)
  other arithmetic  28 us (5%)
  local copies, waits for them, and re-layouts  25.2 us (5%)
  between operations  14.8 us (3%)
  starting transfers between devices  9.86 us (2%)
    psum x1, waiting for transfers between devices, on_device(): lax.psum((running[0], running[1], running[2]), ('row', 'col'))  126 us
    psum x1, blocking collectives, on_device(): lax.psum((running[0], running[1], running[2]), ('row', 'col'))  79.4 us
    unnamed x1, blocking collectives  55 us
    all_gather x1, blocking collectives, picked(): lax.all_gather(value, axis)  52.6 us
    dot_general x36, matrix products, outer(): lax.dot_general(first, second, (((1,), (1,)), ((), ())), preferred_elemen...  34.7 us
    dot_general x24, matrix products, transition(): jnp.dot(hidden, w_out, preferred_element_type=jnp.float32)  27.4 us
    dot_general x12, matrix products, transition(): pre_act = jnp.dot(normed, w_in, preferred_element_type=jnp.float32) + b_in  19.6 us
    div x12, matrix products, pair_backward(): probs = expo / jnp.sum(expo, axis=-1, keepdims=True)  17.9 us
  transfers between devices with their start and end apart: 3, of which 2 were waited for; matrix products, arithmetic and copies ran while one was open for 1% of the time, Pallas kernels for 0%

commit v1 on v0

--- a/solution.py
+++ b/solution.py
@@ -133,7 +133,9 @@
         left_terms.reshape(tile_rows, width), "col", scatter_dimension=0, tiled=True
     )
     grad_right = over_copies(running[3], "row")
-    grad_in, grad_out, grad_bins = lax.psum((running[0], running[1], running[2]), ("row", "col"))
+    grad_in, grad_out, grad_bins = lax.psum(
+        lax.psum((running[0], running[1], running[2]), "col"), "row"
+    )
     residues = tile_rows * lax.axis_size("row")
     return (grad_left, grad_right, grad_in / residues, grad_out / residues, grad_bins / residues)
 

time: 514 us -> 661 us (1.29)
  waiting for transfers between devices: 131 us -> 322 us
  blocking collectives: 187 us -> 136 us
  local copies, waits for them, and re-layouts: 25.2 us -> 33.6 us
    unnamed x1 -> x4, waiting for transfers between devices: 0.02 us -> 122 us
    psum x1 -> x2, waiting for transfers between devices: 126 us -> 195 us  [the longest x1 108 us: on_device(): lax.psum((running[0], running[1], running[2]), 'col')]
    unnamed x1 -> x0, blocking collectives: 55 us -> none
    dynamic_update_slice x12, local copies, waits for them, and re-layouts: 0.09 us -> 7.19 us  [on_device(): running, left_terms = lax.scan(advance, start, records)]
  transfers between devices with their start and end apart: 3 -> 5, of which waited for: 2 -> 4; matrix products, arithmetic and copies ran while one was open for 1% -> 1% of each run, Pallas kernels for 0% -> 0%
where the time goes in v1:
time: 661 us; the launch traced here: 659 us
  waiting for transfers between devices  322 us (49%)
  blocking collectives  136 us (21%)
  matrix products  113 us (17%)
  local copies, waits for them, and re-layouts  33.6 us (5%)
  other arithmetic  28 us (4%)
  between operations  14.5 us (2%)
  starting transfers between devices  9.93 us (2%)
    unnamed x4, waiting for transfers between devices  122 us
    psum x1, waiting for transfers between devices, on_device(): lax.psum((running[0], running[1], running[2]), 'col')  108 us
    psum x1, waiting for transfers between devices, on_device(): lax.psum(lax.psum((running[0], running[1], running[2]), 'col'), 'row')  86.6 us
    psum x1, blocking collectives, on_device(): lax.psum(lax.psum((running[0], running[1], running[2]), 'col'), 'row')  82.9 us
    all_gather x1, blocking collectives, picked(): lax.all_gather(value, axis)  52.6 us
    dot_general x36, matrix products, outer(): lax.dot_general(first, second, (((1,), (1,)), ((), ())), preferred_elemen...  34.6 us
    dot_general x24, matrix products, transition(): jnp.dot(hidden, w_out, preferred_element_type=jnp.float32)  27.3 us
    dot_general x12, matrix products, transition(): pre_act = jnp.dot(normed, w_in, preferred_element_type=jnp.float32) + b_in  19.6 us
  transfers between devices with their start and end apart: 5, of which 4 were waited for; matrix products, arithmetic and copies ran while one was open for 1% of the time, Pallas kernels for 0%

profile of v1, /device:TPU:2, one launch (start us, length us, event | category | flops | bytes accessed | tf_op | source)
XLA Modules:
  0.0 659.4 jit_solution(14587531637248019851)
XLA Ops:
  8.5 6.2 all-to-all-start
  14.8 4.7 all-to-all-done
  19.8 52.6 %all_gather.3 = bf16[16,2,96,128]{3,2,1,0:T(8,128)(2,1)S(1)} all-gather(bf16[1,2,96,128]{3,2,1,0:T(8,128)(2,1)S(1)} %copy.34), channel_id=1, replica_groups=mesh['row'=16,'col'=16] {'row'}, dimensions={0}, use_global_device_ids=true | all-gather | bytes 835584 | tf_op jit(solution)/shard_map/all_gather | solution.py:26
  72.4 167.8 %while.19 = (s32[]{:T(128)}, f32[128,512]{1,0:T(8,128)S(1)}, f32[512,128]{1,0:T(8,128)S(1)}, f32[128,64]{0,1:T(8,128)S(1)}, f32[96,128]{1,0:T(8,128)S(1)}, /*ind...) while((s32[]{:T(128)}, f32[128,512]{1,0:T(8,128)S(1)}, ...), condition=%wide.region_11.12_spmd.clone, body=%wide.region_0.11_spmd.clone.sunk | while | flops 869032064 | bytes 20266860 | solution.py:131
  81.7 2.1 multiply_convert_fusion.6
  88.2 1.9 fusion.121
  95.7 2.1 multiply_convert_fusion.6
  102.2 1.9 fusion.121
  109.7 2.1 multiply_convert_fusion.6
  116.2 1.9 fusion.121
  123.7 2.1 multiply_convert_fusion.6
  137.7 2.1 multiply_convert_fusion.6
  151.7 2.1 multiply_convert_fusion.6
  165.7 2.1 multiply_convert_fusion.6
  179.7 2.1 multiply_convert_fusion.6
  193.6 2.1 multiply_convert_fusion.6
  207.6 2.1 multiply_convert_fusion.6
  221.6 2.1 multiply_convert_fusion.6
  235.6 2.1 multiply_convert_fusion.6
  242.0 3.6 all-to-all-start.1
  246.4 108.0 %all-reduce.10.cloned.1.call-done = (f32[128,512]{1,0:T(8,128)}, f32[512,128]{1,0:T(8,128)}) async-done(((f32[128,512]{1,0:T(8,128)}, f32[512,128]{1,0:T(8,128)}), (f32[128,512]{1,0:T(8,128)}, f32[512,128]{1,0:T(8,128)})) %all-reduce.10.cloned.1.call-update) | async-done | bytes 524304 | tf_op jit(solution)/shard_map/psum | solution.py:137
  355.7 121.6 %all-reduce.8.cloned.1.call-done = (f32[96,128]{1,0:T(8,128)}, f32[128,64]{0,1:T(8,128)}) async-done(((f32[96,128]{1,0:T(8,128)}, f32[128,64]{0,1:T(8,128)}), (f32[96,128]{1,0:T(8,128)}, f32[128,64]{0,1:T(8,128)})) %all-reduce.8.cloned.1.call-update) | async-done | bytes 81936
  477.3 82.9 %psum.47 = f32[128,64]{0,1:T(8,128)S(1)} all-reduce(f32[128,64]{0,1:T(8,128)} %get-tuple-element.234), channel_id=1, replica_groups=mesh['row'=16,'col'=16] {'row'}, use_global_device_ids=true, to_apply=%region_19.20 | all-reduce | flops 8192 | bytes 65536 | tf_op jit(solution)/shard_map/psum | solution.py:136
  562.2 86.6 %all-reduce.12.cloned.1.call-done = (f32[128,512]{1,0:T(8,128)}, f32[512,128]{1,0:T(8,128)}) async-done(((f32[128,512]{1,0:T(8,128)}, f32[512,128]{1,0:T(8,128)}), (f32[128,512]{1,0:T(8,128)}, f32[512,128]{1,0:T(8,128)})) %all-reduce.12.cloned.1.call-update) | async-done | bytes 524304 | tf_op jit(solution)/shard_map/psum | solution.py:136
  (620 shorter events, 144.9 us)
Async XLA Ops:
  8.5 10.9 %all-to-all-start = ((bf16[16,2,6,128]{3,1,2,0:T(2,128)(2,1)}), bf16[16,2,6,128]{3,1,2,0:T(2,128)(2,1)S(1)}, u32[]{:S(2)}, u32[]{:S(2)}) async-start(bf16[16,2,6,128]{3,1,2,0:T(2,128)(2,1)} %broadcast_in_dim.22), calls=%async_computation | async-start | bytes 98304 | tf_op jit(solution)/shard_map/all_to_all | solution.py:9
  14.7 339.7 %all-reduce.10.cloned.1.call-start = ((), (), s32[]{:S(2)}) async-start(), calls=%async_computation.3 | async-start | bytes 1048576 | tf_op jit(solution)/shard_map/psum | solution.py:137
  88.2 2.7 copy-start.2
  88.2 2.7 copy-start.8
  102.2 2.7 copy-start.2
  102.2 2.7 copy-start.8
  116.1 2.7 copy-start.2
  116.2 2.7 copy-start.8
  130.1 2.7 copy-start.2
  130.1 2.7 copy-start.8
  144.1 2.7 copy-start.2
  158.1 2.7 copy-start.2
  158.1 2.7 copy-start.8
  172.1 2.7 copy-start.2
  186.1 2.7 copy-start.2
  200.1 2.7 copy-start.2
  214.1 2.7 copy-start.2
  228.0 2.7 copy-start.2
  228.1 2.7 copy-start.8
  240.2 5.4 copy-start.5
  241.0 113.5 %copy-start.9 = (u32[256]{0:T(256)S(1)}, u32[256]{0:T(256)}, u32[]{:S(2)}) copy-start(u32[256]{0:T(256)} %constant.59) | copy-start | bytes 3076
  242.0 410.2 %all-to-all-start.1 = ((f32[16,96,128]{2,1,0:T(8,128)}), f32[16,96,128]{2,1,0:T(8,128)S(1)}, u32[]{:S(2)}, u32[]{:S(2)}) async-start(f32[16,96,128]{2,1,0:T(8,128)} %broadcast_in_dim.23), calls=%async_computation.1 | async-start | bytes 1572864 | tf_op jit(solution)/shard_map/all_to_all | solution.py:9
  245.6 231.7 %all-reduce.8.cloned.1.call-start = ((), (), s32[]{:S(2)}) async-start(), calls=%async_computation.2 | async-start | bytes 163840
  246.4 402.4 %all-reduce.12.cloned.1.call-start = ((), (), s32[]{:S(2)}) async-start(), calls=%async_computation.4 | async-start | bytes 1048576 | tf_op jit(solution)/shard_map/psum | solution.py:136
  (57 other events, 122.4 us)
Sparse Core Ops, SparseCore 0:
  241.1 113.2 all-reduce.9
  357.7 119.5 all-reduce.7
  480.0 168.7 all-reduce.11
